TPU v7x, 32 devices: a whole 2x2x4 slice. The times are simulated.
32 devices in a mesh: row: 4 (over y, x), col: 8 (over z, core).
Axes of the slice: x: 2, y: 2, z: 4, core: 2. Of those that a mesh axis runs over, the one named last changes fastest.
Arguments:
- charge: float32 [256, 256, 256], P('col', 'row'), may hold values from -6 to 6
- green_spectrum: float32 [512, 512, 512], P('row', 'col'), may hold values from 0.2 to 2
Outputs:
- potential: float32 [256, 256, 256], P('col', 'row')
All inputs are finite; a program needn't handle non-finite values.
Results may differ from a plain program's by a relative error of at most 0.00007.
Values sent between devices are 32-bit elements; how exact they have to be, the bound alone decides.
A program may use at most 192 MiB of HBM per device.

v0:
```python
import math
import jax
import jax.numpy as jnp
from jax import lax
from jax.sharding import PartitionSpec as P

M = 512
N = 256


def phases(count_in, count_out, length):
    row_ids = lax.iota(jnp.int32, count_in)[:, None]
    col_ids = lax.iota(jnp.int32, count_out)[None, :]
    turn_ids = row_ids * col_ids % length
    angles = turn_ids.astype(jnp.float32) * (2.0 * math.pi / length)
    return (jnp.cos(angles), jnp.sin(angles))


def forward_table(count_in, count_out, length):
    cosine, sine_part = phases(count_in, count_out, length)
    return jnp.stack([jnp.stack([cosine, -sine_part], 1), jnp.stack([sine_part, cosine], 1)], 0)


def inverse_table(count_in, count_out, length):
    cosine, sine_part = phases(count_in, count_out, length)
    scaling = 1.0 / length
    return (
        jnp.stack([jnp.stack([cosine, sine_part], 1), jnp.stack([-sine_part, cosine], 1)], 0)
        * scaling
    )


def contract(pattern, left_side, right_side):
    return jnp.einsum(
        pattern,
        left_side,
        right_side,
        precision=lax.Precision.HIGH,
        preferred_element_type=jnp.float32,
    )


def on_device(charge, green_spectrum):
    cosine, sine_part = phases(N, M, M)
    real_table = jnp.stack([cosine, -sine_part], 1)
    along_z = contract("xyz,zqk->xyqk", charge, real_table)
    by_rows = lax.all_to_all(along_z, "row", split_axis=3, concat_axis=1, tiled=True)
    forward = forward_table(N, M, M)
    along_y = contract("xypk,pyqb->xkqb", by_rows, forward)
    spectrum = contract(
        "xkpj,pxqa->kjqa",
        lax.all_to_all(along_y, "col", split_axis=3, concat_axis=0, tiled=True),
        forward,
    )
    product = spectrum * green_spectrum[:, :, None, :]
    back_table = inverse_table(M, N, M)
    back_cos, back_sin = phases(M, N, M)
    real_back = jnp.stack([back_cos, -back_sin], 0) * (1.0 / M)
    back_x = contract("kjqa,qapx->kjpx", product, back_table)
    by_cols = lax.all_to_all(back_x, "col", split_axis=3, concat_axis=1, tiled=True)
    back_y = contract("kbpx,pbqy->kxqy", by_cols, back_table)
    return contract(
        "cxpy,pcz->xyz",
        lax.all_to_all(back_y, "row", split_axis=3, concat_axis=0, tiled=True),
        real_back,
    )


def solution(mesh):
    in_specs = (P("col", "row", None), P("row", "col", None))
    out_specs = P("col", "row", None)
    return jax.shard_map(
        on_device, mesh=mesh, in_specs=in_specs, out_specs=out_specs, check_vma=False
    )
```

profile of v0, /device:TPU:0, one launch (start us, length us, event | category | flops | bytes accessed | tf_op | source)
XLA Modules:
  0.0 1271.5 jit_solution(5702876776140178700)
XLA Ops:
  2.1 5.7 convolution_bitcast_fusion.1
  7.8 16.3 %copy.38 = f32[32,64,2,512]{1,0,2,3:T(8,128)} copy(f32[32,64,2,512]{3,1,0,2:T(8,128)} %convolution_bitcast_fusion.1) | data formatting | bytes 16777216 | tf_op jit(solution)/shard_map/xyz,zqk->xyqk/dot_general | solution.py:34
  24.1 14.3 %reshape.237 = f32[4,1,524288]{2,1,0:T(1,128)} reshape(f32[512,2,32,64]{3,2,1,0:T(8,128)} %bitcast.92) | data formatting | bytes 16777216
  38.5 5.8 all-to-all-start
  46.5 91.6 %all-to-all-done = f32[4,1,524288]{2,1,0:T(1,128)} async-done(((f32[4,1,524288]{2,1,0:T(1,128)}), f32[4,1,524288]{2,1,0:T(1,128)}, u32[]{:S(2)}, u32[]{:S(2)}) %all-to-all-start) | async-done | bytes 8388640 | tf_op jit(solution)/shard_map/all_to_all | solution.py:47
  138.6 28.2 %reduce = f32[4,524288]{1,0:T(4,128)} reduce(f32[4,1,524288]{2,1,0:T(1,128)} %all-to-all-done, f32[]{:T(128)} %broadcast.343), dimensions={1}, to_apply=%all_to_all.52.reduce_sub_computation | reduce | bytes 16777220 | tf_op jit(solution)/shard_map/all_to_all | solution.py:47
  166.8 16.8 %reshape.238 = f32[512,2,32,64]{3,2,1,0:T(8,128)} reshape(f32[4,524288]{1,0:T(4,128)} %reduce) | data formatting | bytes 16777216
  183.6 12.8 %copy.67 = f32[32,64,2,4,128]{4,3,1,2,0:T(4,128)} copy(f32[32,64,2,4,128]{1,0,2,4,3:T(8,128)} %bitcast.93) | data formatting | bytes 16777216 | tf_op jit(solution)/shard_map/all_to_all | solution.py:47
  201.1 16.9 %convolution_bitcast_fusion = f32[32,128,2,512]{3,1,2,0:T(8,128)} fusion(f32[32,256,2,128,1]{3,1,2,4,0:T(8,128)S(1)} %bitcast.99, f32[1,256,2,512]{3,1,2,0:T(8,128)S(1)} %get-tuple-element.8, f32[1,256,2,512]{3,1,2,0:T(8,128)S(1)} %get-tuple-element.7), kind=kOutput, calls=%fused_computation.9 | convolution fusion | flops 12885426176 | bytes 27262976 | tf_op jit(solution)/shard_map/xypk,pyqb->xkqb/dot_general | solution.py:34
  218.0 25.1 %copy.43 = f32[32,128,2,512]{1,2,0,3:T(2,128)} copy(f32[32,128,2,512]{3,1,2,0:T(8,128)} %convolution_bitcast_fusion) | data formatting | bytes 33554432 | tf_op jit(solution)/shard_map/xypk,pyqb->xkqb/dot_general | solution.py:34
  243.0 5.7 all-to-all-start.1
  248.8 17.7 %copy.48 = f32[128,64,512]{2,0,1:T(8,128)} copy(f32[128,64,512]{2,1,0:T(8,128)} %param.3) | data formatting | bytes 33554432 | tf_op args[1]
  271.6 340.8 %all-to-all-done.1 = f32[32,128,2,512]{1,2,0,3:T(2,128)} async-done(((f32[32,128,2,512]{1,2,0,3:T(2,128)}), f32[32,128,2,512]{1,2,0,3:T(2,128)}, u32[]{:S(2)}, u32[]{:S(2)}) %all-to-all-start.1) | async-done | bytes 16777248 | tf_op jit(solution)/shard_map/all_to_all | solution.py:52
  612.4 11.0 copy.44
  625.2 45.0 %fusion.4 = f32[128,64,2,512,1]{3,0,4,2,1:T(8,128)} fusion(f32[256,128,2,64,1]{1,3,2,0,4:T(8,128)S(1)} %bitcast.91, f32[1,256,2,512]{3,1,2,0:T(8,128)S(1)} %get-tuple-element.8, f32[1,256,2,512]{3,1,2,0:T(8,128)S(1)} %get-tuple-element.7), kind=kOutput, calls=%fused_computation.5 | convolution fusion | flops 25770328064 | bytes 52428800 | tf_op jit(solution)/shard_map/xkpj,pxqa->kjqa/dot_general | solution.py:34
  670.3 33.9 %fusion.7 = f32[128,64,2,256]{3,0,2,1:T(8,128)} fusion(f32[128,64,2,512,1]{3,0,4,2,1:T(8,128)} %fusion.4, f32[128,64,512]{2,0,1:T(8,128)} %copy.48, f32[1,512,2,256]{3,1,0,2:T(8,128)S(1)} %copy-done.2, f32[1,512,2,256]{3,1,0,2:T(8,128)S(1)} %get-tuple-element.5), kind=kOutput, calls=%fused_computation.8 | convolution fusion | flops 25779240960 | bytes 69206016 | tf_op jit(solution)/shard_map/kjqa,qapx->kjpx/dot_general | solution.py:34
  704.2 25.1 %copy.50 = f32[128,64,2,256]{0,2,1,3:T(2,128)} copy(f32[128,64,2,256]{3,0,2,1:T(8,128)} %fusion.7) | data formatting | bytes 33554432 | tf_op jit(solution)/shard_map/kjqa,qapx->kjpx/dot_general | solution.py:34
  729.2 367.8 %all_to_all.72 = f32[128,64,2,256]{0,2,1,3:T(2,128)S(1)} all-to-all(f32[128,64,2,256]{0,2,1,3:T(2,128)} %copy.50), channel_id=1, replica_groups=mesh['row'=4,'col'=8] {'col'}, dimensions={3} | all-to-all | bytes 33554432 | tf_op jit(solution)/shard_map/all_to_all | solution.py:60
  1097.0 10.3 copy.51
  1107.3 7.0 copy.52
  1114.3 32.6 %fusion.13 = f32[128,32,2,256]{3,0,2,1:T(8,128)} fusion(f32[128,512,2,32,1]{0,3,2,1,4:T(8,128)} %bitcast.98, f32[1,512,2,256]{3,1,0,2:T(8,128)S(1)} %copy-done.3, f32[1,512,2,256]{3,1,0,2:T(8,128)S(1)} %get-tuple-element.5), kind=kOutput, calls=%fused_computation.13 | convolution fusion | flops 12885950464 | bytes 27262976 | tf_op jit(solution)/shard_map/kbpx,pbqy->kxqy/dot_general | solution.py:34
  1146.9 13.2 %copy.54 = f32[128,32,2,256]{0,2,1,3:T(2,128)} copy(f32[128,32,2,256]{3,0,2,1:T(8,128)} %fusion.13) | data formatting | bytes 16777216 | tf_op jit(solution)/shard_map/kbpx,pbqy->kxqy/dot_general | solution.py:34
  1167.9 90.2 %all-to-all-done.3 = f32[128,32,2,256]{0,2,1,3:T(2,128)} async-done(((f32[128,32,2,256]{0,2,1,3:T(2,128)}), f32[128,32,2,256]{0,2,1,3:T(2,128)}, u32[]{:S(2)}, u32[]{:S(2)}) %all-to-all-start.3) | async-done | bytes 8388640 | tf_op jit(solution)/shard_map/all_to_all | solution.py:64
  1258.1 8.4 copy.55
  (20 shorter events, 29.0 us)
Async XLA Ops:
  0.0 2.1 copy-start
  38.5 99.7 %all-to-all-start = ((f32[4,1,524288]{2,1,0:T(1,128)}), f32[4,1,524288]{2,1,0:T(1,128)}, u32[]{:S(2)}, u32[]{:S(2)}) async-start(f32[4,1,524288]{2,1,0:T(1,128)} %reshape.237), calls=%async_computation | async-start | bytes 16777216 | tf_op jit(solution)/shard_map/all_to_all | solution.py:47
  243.0 369.4 %all-to-all-start.1 = ((f32[32,128,2,512]{1,2,0,3:T(2,128)}), f32[32,128,2,512]{1,2,0,3:T(2,128)}, u32[]{:S(2)}, u32[]{:S(2)}) async-start(f32[32,128,2,512]{1,2,0,3:T(2,128)} %copy.43), calls=%async_computation.1 | async-start | bytes 33554432 | tf_op jit(solution)/shard_map/all_to_all | solution.py:52
  625.2 45.1 %copy-start.2 = (f32[1,512,2,256]{3,1,0,2:T(8,128)S(1)}, f32[1,512,2,256]{3,1,0,2:T(8,128)}, u32[]{:S(2)}) copy-start(f32[1,512,2,256]{3,1,0,2:T(8,128)} %get-tuple-element.6) | copy-start | bytes 3145732
  1107.3 7.0 copy-start.3
  1160.1 97.9 %all-to-all-start.3 = ((f32[128,32,2,256]{0,2,1,3:T(2,128)}), f32[128,32,2,256]{0,2,1,3:T(2,128)}, u32[]{:S(2)}, u32[]{:S(2)}) async-start(f32[128,32,2,256]{0,2,1,3:T(2,128)} %copy.54), calls=%async_computation.3 | async-start | bytes 16777216 | tf_op jit(solution)/shard_map/all_to_all | solution.py:64
  1258.1 13.3 %copy-start.1 = (f32[32,64,256]{2,1,0:T(8,128)S(1)}, f32[32,64,256]{2,1,0:T(8,128)}, u32[]{:S(2)}) copy-start(f32[32,64,256]{2,1,0:T(8,128)} %param.2) | copy-start | bytes 6291460
where the time goes:
time: 1280 us; the launch traced here: 1270 us
  waiting for transfers between devices  523 us (41%)
  blocking collectives  368 us (29%)
  local copies, waits for them, and re-layouts  185 us (14%)
  matrix products  139 us (11%)
  other arithmetic  39.7 us (3%)
  starting transfers between devices  17.2 us (1%)
    all_to_all x1, blocking collectives, on_device(): lax.all_to_all(back_x, 'col', split_axis=3, concat_axis=1, tiled=True)  368 us
    all_to_all x1, waiting for transfers between devices, on_device(): lax.all_to_all(along_y, 'col', split_axis=3, concat_axis=0, tiled=True)  341 us
    dot_general x6, matrix products, contract(): jnp.einsum(pattern, left_side, right_side, precision=lax.Precision.HIGH,...  139 us
    all_to_all x1, waiting for transfers between devices, on_device(): lax.all_to_all(along_z, 'row', split_axis=3, concat_axis=1, tiled=True)  91.6 us
    all_to_all x1, waiting for transfers between devices, on_device(): lax.all_to_all(back_y, 'row', split_axis=3, concat_axis=0, tiled=True)  90.2 us
    dot_general x4, local copies, waits for them, and re-layouts, contract(): jnp.einsum(pattern, left_side, right_side, precision=lax.Precision.HIGH,...  79.7 us
    unnamed x11, local copies, waits for them, and re-layouts  48.9 us
    all_to_all x1, other arithmetic, on_device(): lax.all_to_all(along_z, 'row', split_axis=3, concat_axis=1, tiled=True)  28.2 us
  transfers between devices with their start and end apart: 3, of which 3 were waited for; matrix products, arithmetic and copies ran while one was open for 2% of the time, Pallas kernels for 0%

commit v1 on v0

--- a/solution.py
+++ b/solution.py
@@ -44,7 +44,10 @@
     cosine, sine_part = phases(N, M, M)
     real_table = jnp.stack([cosine, -sine_part], 1)
     along_z = contract("xyz,zqk->xyqk", charge, real_table)
-    by_rows = lax.all_to_all(along_z, "row", split_axis=3, concat_axis=1, tiled=True)
+    by_rows = jnp.concatenate(
+        lax.all_to_all(jnp.stack(jnp.split(along_z, lax.axis_size("row"), axis=3)), "row", 0, 0),
+        axis=1,
+    )
     forward = forward_table(N, M, M)
     along_y = contract("xypk,pyqb->xkqb", by_rows, forward)
     spectrum = contract(

time: 1280 us -> 1190 us (0.930)
  local copies, waits for them, and re-layouts: 185 us -> 125 us
  other arithmetic: 39.7 us -> 15.1 us
    unnamed x11 -> x9, local copies, waits for them, and re-layouts: 48.9 us -> 17.7 us
    all_to_all x1 -> x0, other arithmetic: 28.2 us -> none  [on_device(): lax.all_to_all(along_z, 'row', split_axis=3, concat_axis=1, tiled=True)]
    all_to_all x3 -> x0, local copies, waits for them, and re-layouts: 18 us -> none  [on_device(): lax.all_to_all(along_z, 'row', split_axis=3, concat_axis=1, tiled=True)]
    dot_general x4 -> x3, local copies, waits for them, and re-layouts: 79.7 us -> 63.3 us  [contract(): jnp.einsum(pattern, left_side, right_side, precision=lax.Precision.HIGH,...]
where the time goes in v1:
time: 1190 us; the launch traced here: 1180 us
  waiting for transfers between devices  523 us (44%)
  blocking collectives  368 us (31%)
  matrix products  137 us (12%)
  local copies, waits for them, and re-layouts  125 us (11%)
  starting transfers between devices  17.5 us (1%)
  other arithmetic  15.1 us (1%)
    all_to_all x1, blocking collectives, on_device(): lax.all_to_all(back_x, 'col', split_axis=3, concat_axis=1, tiled=True)  368 us
    all_to_all x1, waiting for transfers between devices, on_device(): lax.all_to_all(along_y, 'col', split_axis=3, concat_axis=0, tiled=True)  341 us
    dot_general x6, matrix products, contract(): jnp.einsum(pattern, left_side, right_side, precision=lax.Precision.HIGH,...  137 us
    all_to_all x1, waiting for transfers between devices, on_device(): lax.all_to_all(jnp.stack(jnp.split(along_z, lax.axis_size('row'), axis=3)...  91.6 us
    all_to_all x1, waiting for transfers between devices, on_device(): lax.all_to_all(back_y, 'row', split_axis=3, concat_axis=0, tiled=True)  90.2 us
    dot_general x3, local copies, waits for them, and re-layouts, contract(): jnp.einsum(pattern, left_side, right_side, precision=lax.Precision.HIGH,...  63.3 us
  transfers between devices with their start and end apart: 3, of which 3 were waited for; matrix products, arithmetic and copies ran while one was open for 2% of the time, Pallas kernels for 0%

profile of v1, /device:TPU:0, one launch (start us, length us, event | category | flops | bytes accessed | tf_op | source)
XLA Modules:
  0.0 1184.8 jit_solution(134787478060688913)
XLA Ops:
  2.1 3.7 convolution_bitcast_fusion.1
  6.7 3.6 pad_maximum_fusion
  10.4 5.8 all-to-all-start
  18.4 91.6 %all-to-all-done = f32[4,32,64,2,128]{4,2,1,3,0:T(8,128)} async-done(((f32[4,32,64,2,128]{4,2,1,3,0:T(8,128)}), f32[4,32,64,2,128]{4,2,1,3,0:T(8,128)}, u32[]{:S(2)}, u32[]{:S(2)}) %all-to-all-start) | async-done | bytes 8388640 | tf_op jit(solution)/shard_map/all_to_all | solution.py:48
  110.1 4.2 copy.20
  114.3 16.5 %convolution_bitcast_fusion = f32[32,128,2,512]{3,1,2,0:T(8,128)} fusion(f32[32,256,2,128,1]{3,1,2,4,0:T(8,128)S(1)} %bitcast.101, f32[1,256,2,512]{3,1,2,0:T(8,128)S(1)} %get-tuple-element.12, f32[1,256,2,512]{3,1,2,0:T(8,128)S(1)} %get-tuple-element.11), kind=kOutput, calls=%fused_computation.9 | convolution fusion | flops 12885426176 | bytes 27262976 | tf_op jit(solution)/shard_map/xypk,pyqb->xkqb/dot_general | solution.py:34
  130.8 25.1 %copy.23 = f32[32,128,2,512]{1,2,0,3:T(2,128)} copy(f32[32,128,2,512]{3,1,2,0:T(8,128)} %convolution_bitcast_fusion) | data formatting | bytes 33554432 | tf_op jit(solution)/shard_map/xypk,pyqb->xkqb/dot_general | solution.py:34
  155.8 6.0 all-to-all-start.1
  161.8 17.7 %copy.28 = f32[128,64,512]{2,0,1:T(8,128)} copy(f32[128,64,512]{2,1,0:T(8,128)} %param.3) | data formatting | bytes 33554432 | tf_op args[1]
  184.7 340.8 %all-to-all-done.1 = f32[32,128,2,512]{1,2,0,3:T(2,128)} async-done(((f32[32,128,2,512]{1,2,0,3:T(2,128)}), f32[32,128,2,512]{1,2,0,3:T(2,128)}, u32[]{:S(2)}, u32[]{:S(2)}) %all-to-all-start.1) | async-done | bytes 16777248 | tf_op jit(solution)/shard_map/all_to_all | solution.py:55
  525.5 11.0 copy.24
  538.3 45.3 %fusion.4 = f32[128,64,2,512,1]{3,0,4,2,1:T(8,128)} fusion(f32[256,128,2,64,1]{1,3,2,0,4:T(8,128)S(1)} %bitcast.96, f32[1,256,2,512]{3,1,2,0:T(8,128)S(1)} %get-tuple-element.12, f32[1,256,2,512]{3,1,2,0:T(8,128)S(1)} %get-tuple-element.11), kind=kOutput, calls=%fused_computation.5 | convolution fusion | flops 25770328064 | bytes 52428800 | tf_op jit(solution)/shard_map/xkpj,pxqa->kjqa/dot_general | solution.py:34
  583.6 33.8 %fusion.7 = f32[128,64,2,256]{3,0,2,1:T(8,128)} fusion(f32[128,64,2,512,1]{3,0,4,2,1:T(8,128)} %fusion.4, f32[128,64,512]{2,0,1:T(8,128)} %copy.28, f32[1,512,2,256]{3,1,0,2:T(8,128)S(1)} %copy-done.2, f32[1,512,2,256]{3,1,0,2:T(8,128)S(1)} %get-tuple-element.9), kind=kOutput, calls=%fused_computation.8 | convolution fusion | flops 25779240960 | bytes 69206016 | tf_op jit(solution)/shard_map/kjqa,qapx->kjpx/dot_general | solution.py:34
  617.4 25.0 %copy.30 = f32[128,64,2,256]{0,2,1,3:T(2,128)} copy(f32[128,64,2,256]{3,0,2,1:T(8,128)} %fusion.7) | data formatting | bytes 33554432 | tf_op jit(solution)/shard_map/kjqa,qapx->kjpx/dot_general | solution.py:34
  642.4 367.8 %all_to_all.59 = f32[128,64,2,256]{0,2,1,3:T(2,128)S(1)} all-to-all(f32[128,64,2,256]{0,2,1,3:T(2,128)} %copy.30), channel_id=1, replica_groups=mesh['row'=4,'col'=8] {'col'}, dimensions={3} | all-to-all | bytes 33554432 | tf_op jit(solution)/shard_map/all_to_all | solution.py:63
  1010.1 10.3 copy.31
  1020.4 7.0 copy.32
  1027.4 32.5 %fusion.13 = f32[128,32,2,256]{3,0,2,1:T(8,128)} fusion(f32[128,512,2,32,1]{0,3,2,1,4:T(8,128)} %bitcast.100, f32[1,512,2,256]{3,1,0,2:T(8,128)S(1)} %copy-done.3, f32[1,512,2,256]{3,1,0,2:T(8,128)S(1)} %get-tuple-element.9), kind=kOutput, calls=%fused_computation.14 | convolution fusion | flops 12885950464 | bytes 27262976 | tf_op jit(solution)/shard_map/kbpx,pbqy->kxqy/dot_general | solution.py:34
  1059.9 13.2 %copy.34 = f32[128,32,2,256]{0,2,1,3:T(2,128)} copy(f32[128,32,2,256]{3,0,2,1:T(8,128)} %fusion.13) | data formatting | bytes 16777216 | tf_op jit(solution)/shard_map/kbpx,pbqy->kxqy/dot_general | solution.py:34
  1073.2 5.7 all-to-all-start.3
  1078.8 2.1 sine_negate_fusion
  1080.9 90.2 %all-to-all-done.3 = f32[128,32,2,256]{0,2,1,3:T(2,128)} async-done(((f32[128,32,2,256]{0,2,1,3:T(2,128)}), f32[128,32,2,256]{0,2,1,3:T(2,128)}, u32[]{:S(2)}, u32[]{:S(2)}) %all-to-all-start.3) | async-done | bytes 8388640 | tf_op jit(solution)/shard_map/all_to_all | solution.py:67
  1171.1 8.4 copy.35
  1179.5 4.9 fusion.22
  (16 shorter events, 12.2 us)
Async XLA Ops:
  0.0 2.1 copy-start
  10.4 99.7 %all-to-all-start = ((f32[4,32,64,2,128]{4,2,1,3,0:T(8,128)}), f32[4,32,64,2,128]{4,2,1,3,0:T(8,128)}, u32[]{:S(2)}, u32[]{:S(2)}) async-start(f32[4,32,64,2,128]{4,2,1,3,0:T(8,128)} %pad_maximum_fusion), calls=%async_computation | async-start | bytes 16777216 | tf_op jit(solution)/shard_map/all_to_all | solution.py:48
  155.8 369.6 %all-to-all-start.1 = ((f32[32,128,2,512]{1,2,0,3:T(2,128)}), f32[32,128,2,512]{1,2,0,3:T(2,128)}, u32[]{:S(2)}, u32[]{:S(2)}) async-start(f32[32,128,2,512]{1,2,0,3:T(2,128)} %copy.23), calls=%async_computation.1 | async-start | bytes 33554432 | tf_op jit(solution)/shard_map/all_to_all | solution.py:55
  538.2 45.3 %copy-start.2 = (f32[1,512,2,256]{3,1,0,2:T(8,128)S(1)}, f32[1,512,2,256]{3,1,0,2:T(8,128)}, u32[]{:S(2)}) copy-start(f32[1,512,2,256]{3,1,0,2:T(8,128)} %get-tuple-element.10) | copy-start | bytes 3145732
  1020.4 7.0 copy-start.3
  1073.2 97.9 %all-to-all-start.3 = ((f32[128,32,2,256]{0,2,1,3:T(2,128)}), f32[128,32,2,256]{0,2,1,3:T(2,128)}, u32[]{:S(2)}, u32[]{:S(2)}) async-start(f32[128,32,2,256]{0,2,1,3:T(2,128)} %copy.34), calls=%async_computation.3 | async-start | bytes 16777216 | tf_op jit(solution)/shard_map/all_to_all | solution.py:67
  1171.1 13.3 %copy-start.1 = (f32[32,64,256]{2,1,0:T(8,128)S(1)}, f32[32,64,256]{2,1,0:T(8,128)}, u32[]{:S(2)}) copy-start(f32[32,64,256]{2,1,0:T(8,128)} %param.2) | copy-start | bytes 6291460
